TPU v7x, 32 devices: a whole 2x2x4 slice. The times are simulated.
32 devices in a mesh: gx: 4 (over z), gy: 4 (over y, core), gz: 2 (over x).
Axes of the slice: x: 2, y: 2, z: 4, core: 2. Of those that a mesh axis runs over, the one named last changes fastest.
Arguments:
- volume: bfloat16 [32, 64, 32, 128], P('gx', 'gy', 'gz'), may hold values from -6 to 6
- w_full: bfloat16 [3, 3, 3, 128, 128], replicated, may hold values from -0.15625 to 0.15625
- w_half: bfloat16 [3, 3, 3, 128, 256], replicated, may hold values from -0.15625 to 0.15625
- w_bottom_in: bfloat16 [3, 3, 3, 256, 512], P(None, None, None, None, 'gx'), may hold values from -0.109375 to 0.109375
- w_bottom_out: bfloat16 [3, 3, 3, 512, 512], P(None, None, None, None, 'gx'), may hold values from -0.078125 to 0.078125
- w_up: bfloat16 [3, 3, 3, 768, 256], replicated, may hold values from -0.0625 to 0.0625
Outputs:
- decoded: bfloat16 [16, 32, 16, 256], P('gx', 'gy', 'gz')
All inputs are finite; a program needn't handle non-finite values.
Results may differ from a plain program's by a relative error of at most 0.009.
Values may be sent and summed in bfloat16 or wider, within the bound.
A program may use at most 64 MiB of HBM per device.

v0:
```python
import jax
import jax.numpy as jnp
from jax import lax
from jax.sharding import PartitionSpec as P


def with_halo(cells, sides, width):
    for axis, dim in sides:
        count = lax.axis_size(axis)
        ends = count - 1
        head = lax.slice_in_dim(cells, 0, width, axis=dim)
        tail = lax.slice_in_dim(cells, cells.shape[dim] - width, cells.shape[dim], axis=dim)
        cells = jnp.concatenate(
            [
                lax.ppermute(tail, axis, [(i, (i + 1) % count) for i in range(ends)]),
                cells,
                lax.ppermute(head, axis, [((i + 1) % count, i) for i in range(ends)]),
            ],
            axis=dim,
        )
    return cells


def convolve(padded, kernel):
    size_x = padded.shape[0] - 2
    size_y = padded.shape[1] - 2
    size_z = padded.shape[2] - 2
    channels = padded.shape[3]
    total = jnp.zeros((size_x * size_y * size_z, kernel.shape[4]), jnp.float32)
    for offset_x in range(3):
        for offset_y in range(3):
            for offset_z in range(3):
                window = padded[
                    offset_x : offset_x + size_x,
                    offset_y : offset_y + size_y,
                    offset_z : offset_z + size_z,
                    :,
                ]
                total = total + jnp.dot(
                    window.reshape(-1, channels),
                    kernel[offset_x, offset_y, offset_z],
                    preferred_element_type=jnp.float32,
                )
    return total.reshape(size_x, size_y, size_z, kernel.shape[4])


def rectify(total):
    return jnp.maximum(total, 0.0).astype(jnp.bfloat16)


def shrink(field):
    size_x, size_y, size_z, channels = field.shape
    blocks = field.reshape(size_x // 2, 2, size_y // 2, 2, size_z // 2, 2, channels)
    return jnp.max(blocks, axis=(1, 3, 5))


def enlarge(field):
    size_x, size_y, size_z, channels = field.shape
    spread = jnp.broadcast_to(
        field[:, None, :, None, :, None, :], (size_x, 2, size_y, 2, size_z, 2, channels)
    )
    return spread.reshape(2 * size_x, 2 * size_y, 2 * size_z, channels)


def pad_first(field):
    return jnp.pad(field, ((1, 1), (0, 0), (0, 0), (0, 0)))


def on_device(volume, w_full, w_half, w_bottom_in, w_bottom_out, w_up):
    padded = with_halo(volume, (("gx", 0), ("gy", 1), ("gz", 2)), 1)
    full_level = rectify(convolve(padded, w_full))
    pooled = shrink(full_level)
    pooled_rim = with_halo(pooled, (("gx", 0), ("gy", 1), ("gz", 2)), 1)
    skip_level = rectify(convolve(pooled_rim, w_half))
    coarse = shrink(skip_level)
    column = lax.all_gather(coarse, "gx", axis=0, tiled=True)
    column = with_halo(column, (("gy", 1), ("gz", 2)), 1)
    bottom_first = rectify(convolve(pad_first(column), w_bottom_in))
    filters = lax.all_gather(bottom_first, "gx", axis=3, tiled=True)
    filters = with_halo(filters, (("gy", 1), ("gz", 2)), 1)
    bottom_second = rectify(convolve(pad_first(filters), w_bottom_out))
    regrouped = lax.all_to_all(bottom_second, "gx", split_axis=0, concat_axis=3, tiled=True)
    joined = jnp.concatenate([enlarge(regrouped), skip_level], axis=3)
    joined = with_halo(joined, (("gx", 0), ("gy", 1), ("gz", 2)), 1)
    return convolve(joined, w_up).astype(jnp.bfloat16)


def solution(mesh):
    return jax.shard_map(
        on_device,
        mesh=mesh,
        in_specs=(
            P("gx", "gy", "gz", None),
            P(),
            P(),
            P(None, None, None, None, "gx"),
            P(None, None, None, None, "gx"),
            P(),
        ),
        out_specs=P("gx", "gy", "gz", None),
        check_vma=False,
    )
```

profile of v0, /device:TPU:3, one launch (start us, length us, event | category | flops | bytes accessed | tf_op | source)
XLA Modules:
  0.0 225.7 jit_solution(15556953054492281344)
XLA Ops:
  0.9 3.2 %collective-permute-start = (bf16[1,16,16,128]{3,2,1,0:T(8,128)(2,1)S(1)}, bf16[1,16,16,128]{3,2,1,0:T(8,128)(2,1)S(1)}, u32[]{:S(2)}, u32[]{:S(2)}) collective-permute-start(bf16[1,16,16,128]{3,2,1,0:T(8,128)(2,1)S(1)} %get-tuple-element.74), channel_id=1, source_target_pairs={{0,8},{8,16},{16,24},{1,9},{9,17},{17,25},{2,10},{10,18},{18,26},{... | collective-permute-start | bytes 196616 | tf_op jit(solution)/shard_map/ppermute | solution.py:15
  5.4 3.7 %collective-permute-done.1 = bf16[1,16,16,128]{3,2,1,0:T(8,128)(2,1)S(1)} collective-permute-done((bf16[1,16,16,128]{3,2,1,0:T(8,128)(2,1)S(1)}, bf16[1,16,16,128]{3,2,1,0:T(8,128)(2,1)S(1)}, u32[]{:S(2)}, u32[]{:S(2)}) %collective-permute-start.1) | collective-permute-done | bytes 65568 | tf_op jit(solution)/shard_map/ppermute | solution.py:17
  11.0 5.1 %collective-permute-start.2 = (bf16[10,1,16,128]{3,2,1,0:T(8,128)(2,1)S(1)}, bf16[10,1,16,128]{3,2,1,0:T(8,128)(2,1)S(1)}, u32[]{:S(2)}, u32[]{:S(2)}) collective-permute-start(bf16[10,1,16,128]{3,2,1,0:T(8,128)(2,1)S(1)} %get-tuple-element.64), channel_id=1, source_target_pairs={{0,2},{2,4},{4,6},{1,3},{3,5},{5,7},{8,10},{10,12},{12,14},{9,11},... | collective-permute-start | bytes 122888 | tf_op jit(solution)/shard_map/ppermute | solution.py:15
  18.0 3.4 %collective-permute-done.3 = bf16[10,1,16,128]{3,2,1,0:T(8,128)(2,1)S(1)} collective-permute-done((bf16[10,1,16,128]{3,2,1,0:T(8,128)(2,1)S(1)}, bf16[10,1,16,128]{3,2,1,0:T(8,128)(2,1)S(1)}, u32[]{:S(2)}, u32[]{:S(2)}) %collective-permute-start.3) | collective-permute-done | bytes 40992 | tf_op jit(solution)/shard_map/ppermute | solution.py:17
  22.9 4.1 %collective-permute-start.5 = (bf16[10,18,1,128]{3,2,1,0:T(2,128)(2,1)S(1)}, bf16[10,18,1,128]{3,2,1,0:T(2,128)(2,1)S(1)}, u32[]{:S(2)}, u32[]{:S(2)}) collective-permute-start(bf16[10,18,1,128]{3,2,1,0:T(2,128)(2,1)S(1)} %get-tuple-element.48), channel_id=1, source_target_pairs={{1,0},{3,2},{5,4},{7,6},{9,8},{11,10},{13,12},{15,14},{17,16},{19,... | collective-permute-start | bytes 138248 | tf_op jit(solution)/shard_map/ppermute | solution.py:17
  29.5 2.6 %fusion.380 = (bf16[8,16,16,128]{3,2,1,0:T(8,128)(2,1)S(1)}, bf16[8,16,16,128]{3,2,1,0:T(8,128)(2,1)S(1)}, bf16[8,16,16,128]{3,2,1,0:T(8,128)(2,1)S(1)}, bf16[8,...) fusion(bf16[10,18,17,128]{3,2,1,0:T(8,128)(2,1)S(1)} %get-tuple, ...), kind=kLoop, calls=%fused_computation.565 | loop fusion | bytes 18874368 | tf_op jit(solution)/shard_map/slice | solution.py:33
  41.0 3.2 %collective-permute-start.6 = (bf16[1,8,8,128]{3,2,1,0:T(8,128)(2,1)S(1)}, bf16[1,8,8,128]{3,2,1,0:T(8,128)(2,1)S(1)}, u32[]{:S(2)}, u32[]{:S(2)}) collective-permute-start(bf16[1,8,8,128]{3,2,1,0:T(8,128)(2,1)S(1)} %get-tuple-element.181), channel_id=1, source_target_pairs={{0,8},{8,16},{16,24},{1,9},{9,17},{17,25},{2,10},{10,18},{18,26},{... | collective-permute-start | bytes 49160 | tf_op jit(solution)/shard_map/ppermute | solution.py:15
  45.5 3.2 %collective-permute-done.7 = bf16[1,8,8,128]{3,2,1,0:T(8,128)(2,1)S(1)} collective-permute-done((bf16[1,8,8,128]{3,2,1,0:T(8,128)(2,1)S(1)}, bf16[1,8,8,128]{3,2,1,0:T(8,128)(2,1)S(1)}, u32[]{:S(2)}, u32[]{:S(2)}) %collective-permute-start.7) | collective-permute-done | bytes 16416 | tf_op jit(solution)/shard_map/ppermute | solution.py:17
  48.7 4.5 %collective-permute-start.8 = (bf16[6,1,8,128]{3,2,1,0:T(8,128)(2,1)S(1)}, bf16[6,1,8,128]{3,2,1,0:T(8,128)(2,1)S(1)}, u32[]{:S(2)}, u32[]{:S(2)}) collective-permute-start(bf16[6,1,8,128]{3,2,1,0:T(8,128)(2,1)S(1)} %get-tuple-element.172), channel_id=1, source_target_pairs={{0,2},{2,4},{4,6},{1,3},{3,5},{5,7},{8,10},{10,12},{12,14},{9,11},... | collective-permute-start | bytes 36872 | tf_op jit(solution)/shard_map/ppermute | solution.py:15
  55.1 3.1 %collective-permute-done.9 = bf16[6,1,8,128]{3,2,1,0:T(8,128)(2,1)S(1)} collective-permute-done((bf16[6,1,8,128]{3,2,1,0:T(8,128)(2,1)S(1)}, bf16[6,1,8,128]{3,2,1,0:T(8,128)(2,1)S(1)}, u32[]{:S(2)}, u32[]{:S(2)}) %collective-permute-start.9) | collective-permute-done | bytes 12320 | tf_op jit(solution)/shard_map/ppermute | solution.py:17
  59.6 4.0 %collective-permute-start.11 = (bf16[6,10,1,128]{3,2,1,0:T(2,128)(2,1)S(1)}, bf16[6,10,1,128]{3,2,1,0:T(2,128)(2,1)S(1)}, u32[]{:S(2)}, u32[]{:S(2)}) collective-permute-start(bf16[6,10,1,128]{3,2,1,0:T(2,128)(2,1)S(1)} %get-tuple-element.158), channel_id=1, source_target_pairs={{1,0},{3,2},{5,4},{7,6},{9,8},{11,10},{13,12},{15,14},{17,16},{19,... | collective-permute-start | bytes 46088 | tf_op jit(solution)/shard_map/ppermute | solution.py:17
  69.8 10.3 %all_gather.6 = bf16[8,4,4,256]{3,2,1,0:T(4,128)(2,1)S(1)} all-gather(bf16[2,4,4,256]{3,2,1,0:T(4,128)(2,1)S(1)} %reduce_max.19), channel_id=1, replica_groups=mesh['gx'=4,'gy'=4,'gz'=2] {'gx'}, dimensions={0}, use_global_device_ids=true | all-gather | bytes 81920 | tf_op jit(solution)/shard_map/all_gather | solution.py:76
  80.1 5.9 %collective-permute-start.12 = (bf16[8,1,4,256]{3,2,1,0:T(4,128)(2,1)S(1)}, bf16[8,1,4,256]{3,2,1,0:T(4,128)(2,1)S(1)}, u32[]{:S(2)}, u32[]{:S(2)}) collective-permute-start(bf16[8,1,4,256]{3,2,1,0:T(4,128)(2,1)S(1)} %get-tuple-element.178), channel_id=1, source_target_pairs={{0,2},{2,4},{4,6},{1,3},{3,5},{5,7},{8,10},{10,12},{12,14},{9,11},... | collective-permute-start | bytes 49160 | tf_op jit(solution)/shard_map/ppermute | solution.py:15
  88.2 3.1 %collective-permute-done.13 = bf16[8,1,4,256]{3,2,1,0:T(4,128)(2,1)S(1)} collective-permute-done((bf16[8,1,4,256]{3,2,1,0:T(4,128)(2,1)S(1)}, bf16[8,1,4,256]{3,2,1,0:T(4,128)(2,1)S(1)}, u32[]{:S(2)}, u32[]{:S(2)}) %collective-permute-start.13) | collective-permute-done | bytes 16416 | tf_op jit(solution)/shard_map/ppermute | solution.py:17
  92.9 4.0 %collective-permute-start.15 = (bf16[8,6,1,256]{3,2,1,0:T(2,128)(2,1)S(1)}, bf16[8,6,1,256]{3,2,1,0:T(2,128)(2,1)S(1)}, u32[]{:S(2)}, u32[]{:S(2)}) collective-permute-start(bf16[8,6,1,256]{3,2,1,0:T(2,128)(2,1)S(1)} %get-tuple-element.169), channel_id=1, source_target_pairs={{1,0},{3,2},{5,4},{7,6},{9,8},{11,10},{13,12},{15,14},{17,16},{19,... | collective-permute-start | bytes 73736 | tf_op jit(solution)/shard_map/ppermute | solution.py:17
  112.6 8.5 %all_gather.7 = bf16[8,4,4,512]{3,2,1,0:T(4,128)(2,1)S(1)} all-gather(bf16[8,4,4,128]{3,2,1,0:T(4,128)(2,1)S(1)} %bitcast.716), channel_id=1, replica_groups=mesh['gx'=4,'gy'=4,'gz'=2] {'gx'}, dimensions={3}, use_global_device_ids=true | all-gather | bytes 163840 | tf_op jit(solution)/shard_map/all_gather | solution.py:79
  121.1 4.8 %collective-permute-start.16 = (bf16[8,1,4,512]{3,2,1,0:T(4,128)(2,1)S(1)}, bf16[8,1,4,512]{3,2,1,0:T(4,128)(2,1)S(1)}, u32[]{:S(2)}, u32[]{:S(2)}) collective-permute-start(bf16[8,1,4,512]{3,2,1,0:T(4,128)(2,1)S(1)} %get-tuple-element.154), channel_id=1, source_target_pairs={{0,2},{2,4},{4,6},{1,3},{3,5},{5,7},{8,10},{10,12},{12,14},{9,11},... | collective-permute-start | bytes 98312 | tf_op jit(solution)/shard_map/ppermute | solution.py:15
  127.9 3.3 %collective-permute-done.17 = bf16[8,1,4,512]{3,2,1,0:T(4,128)(2,1)S(1)} collective-permute-done((bf16[8,1,4,512]{3,2,1,0:T(4,128)(2,1)S(1)}, bf16[8,1,4,512]{3,2,1,0:T(4,128)(2,1)S(1)}, u32[]{:S(2)}, u32[]{:S(2)}) %collective-permute-start.17) | collective-permute-done | bytes 32800 | tf_op jit(solution)/shard_map/ppermute | solution.py:17
  132.8 4.0 %collective-permute-start.19 = (bf16[8,6,1,512]{3,2,1,0:T(2,128)(2,1)S(1)}, bf16[8,6,1,512]{3,2,1,0:T(2,128)(2,1)S(1)}, u32[]{:S(2)}, u32[]{:S(2)}) collective-permute-start(bf16[8,6,1,512]{3,2,1,0:T(2,128)(2,1)S(1)} %get-tuple-element.143), channel_id=1, source_target_pairs={{1,0},{3,2},{5,4},{7,6},{9,8},{11,10},{13,12},{15,14},{17,16},{19,... | collective-permute-start | bytes 147464 | tf_op jit(solution)/shard_map/ppermute | solution.py:17
  143.5 2.6 %pad_maximum_fusion.20 = (bf16[8,4,4,512]{3,2,1,0:T(4,128)(2,1)S(1)}, bf16[8,4,4,512]{3,2,1,0:T(4,128)(2,1)}, bf16[8,4,4,512]{3,2,1,0:T(4,128)(2,1)S(1)}, bf16[8...) fusion(bf16[8,6,4,512]{3,2,1,0:T(4,128)(2,1)S(1)} %constant_dynamic-update-slice, ...), kind=kLoop, calls=%fused_computation.288 | loop fusion | flops 1572864 | bytes 1081344 | tf_op jit(solution)/shard_map/concatenate | solution.py:13
  176.4 6.9 %all_to_all.15 = bf16[8,4,4,128]{3,2,1,0:T(4,128)(2,1)S(1)} all-to-all(bf16[8,4,4,128]{3,2,1,0:T(4,128)(2,1)S(1)} %bitcast.718), channel_id=1, replica_groups=mesh['gx'=4,'gy'=4,'gz'=2] {'gx'}, dimensions={0} | all-to-all | bytes 65536 | tf_op jit(solution)/shard_map/all_to_all | solution.py:82
  188.7 3.8 %collective-permute-done.21 = bf16[1,8,8,768]{3,2,1,0:T(8,128)(2,1)S(1)} collective-permute-done((bf16[1,8,8,768]{3,2,1,0:T(8,128)(2,1)S(1)}, bf16[1,8,8,768]{3,2,1,0:T(8,128)(2,1)S(1)}, u32[]{:S(2)}, u32[]{:S(2)}) %collective-permute-start.21) | collective-permute-done | bytes 98336 | tf_op jit(solution)/shard_map/ppermute | solution.py:17
  193.9 4.0 %collective-permute-start.22 = (bf16[6,1,8,768]{3,2,1,0:T(8,128)(2,1)S(1)}, bf16[6,1,8,768]{3,2,1,0:T(8,128)(2,1)S(1)}, u32[]{:S(2)}, u32[]{:S(2)}) collective-permute-start(bf16[6,1,8,768]{3,2,1,0:T(8,128)(2,1)S(1)} %get-tuple-element.68), channel_id=1, source_target_pairs={{0,2},{2,4},{4,6},{1,3},{3,5},{5,7},{8,10},{10,12},{12,14},{9,11},... | collective-permute-start | bytes 221192 | tf_op jit(solution)/shard_map/ppermute | solution.py:15
  205.1 4.2 %collective-permute-start.25 = (bf16[6,10,1,768]{3,2,1,0:T(2,128)(2,1)S(1)}, bf16[6,10,1,768]{3,2,1,0:T(2,128)(2,1)S(1)}, u32[]{:S(2)}, u32[]{:S(2)}) collective-permute-start(bf16[6,10,1,768]{3,2,1,0:T(2,128)(2,1)S(1)} %get-tuple-element.43), channel_id=1, source_target_pairs={{1,0},{3,2},{5,4},{7,6},{9,8},{11,10},{13,12},{15,14},{17,16},{19,... | collective-permute-start | bytes 276488 | tf_op jit(solution)/shard_map/ppermute | solution.py:17
  (303 shorter events, 118.5 us)
Async XLA Ops:
  0.9 4.5 %collective-permute-start = (bf16[1,16,16,128]{3,2,1,0:T(8,128)(2,1)S(1)}, bf16[1,16,16,128]{3,2,1,0:T(8,128)(2,1)S(1)}, u32[]{:S(2)}, u32[]{:S(2)}) collective-permute-start(bf16[1,16,16,128]{3,2,1,0:T(8,128)(2,1)S(1)} %get-tuple-element.74), channel_id=1, source_target_pairs={{0,8},{8,16},{16,24},{1,9},{9,17},{17,25},{2,10},{10,18},{18,26},{... | collective-permute-start | bytes 196616 | tf_op jit(solution)/shard_map/ppermute | solution.py:15
  4.1 5.0 %collective-permute-start.1 = (bf16[1,16,16,128]{3,2,1,0:T(8,128)(2,1)S(1)}, bf16[1,16,16,128]{3,2,1,0:T(8,128)(2,1)S(1)}, u32[]{:S(2)}, u32[]{:S(2)}) collective-permute-start(bf16[1,16,16,128]{3,2,1,0:T(8,128)(2,1)S(1)} %get-tuple-element.73), channel_id=1, source_target_pairs={{8,0},{16,8},{24,16},{9,1},{17,9},{25,17},{10,2},{18,10},{26,18},{... | collective-permute-start | bytes 196616 | tf_op jit(solution)/shard_map/ppermute | solution.py:17
  11.0 7.1 %collective-permute-start.2 = (bf16[10,1,16,128]{3,2,1,0:T(8,128)(2,1)S(1)}, bf16[10,1,16,128]{3,2,1,0:T(8,128)(2,1)S(1)}, u32[]{:S(2)}, u32[]{:S(2)}) collective-permute-start(bf16[10,1,16,128]{3,2,1,0:T(8,128)(2,1)S(1)} %get-tuple-element.64), channel_id=1, source_target_pairs={{0,2},{2,4},{4,6},{1,3},{3,5},{5,7},{8,10},{10,12},{12,14},{9,11},... | collective-permute-start | bytes 122888 | tf_op jit(solution)/shard_map/ppermute | solution.py:15
  16.1 5.3 %collective-permute-start.3 = (bf16[10,1,16,128]{3,2,1,0:T(8,128)(2,1)S(1)}, bf16[10,1,16,128]{3,2,1,0:T(8,128)(2,1)S(1)}, u32[]{:S(2)}, u32[]{:S(2)}) collective-permute-start(bf16[10,1,16,128]{3,2,1,0:T(8,128)(2,1)S(1)} %get-tuple-element.65), channel_id=1, source_target_pairs={{2,0},{4,2},{6,4},{3,1},{5,3},{7,5},{10,8},{12,10},{14,12},{11,9},... | collective-permute-start | bytes 122888 | tf_op jit(solution)/shard_map/ppermute | solution.py:17
  21.6 6.0 %collective-permute-start.4 = (bf16[10,18,1,128]{3,2,1,0:T(2,128)(2,1)S(1)}, bf16[10,18,1,128]{3,2,1,0:T(2,128)(2,1)S(1)}, u32[]{:S(2)}, u32[]{:S(2)}) collective-permute-start(bf16[10,18,1,128]{3,2,1,0:T(2,128)(2,1)S(1)} %get-tuple-element.47), channel_id=1, source_target_pairs={{0,1},{2,3},{4,5},{6,7},{8,9},{10,11},{12,13},{14,15},{16,17},{18,... | collective-permute-start | bytes 138248 | tf_op jit(solution)/shard_map/ppermute | solution.py:15
  22.9 5.7 %collective-permute-start.5 = (bf16[10,18,1,128]{3,2,1,0:T(2,128)(2,1)S(1)}, bf16[10,18,1,128]{3,2,1,0:T(2,128)(2,1)S(1)}, u32[]{:S(2)}, u32[]{:S(2)}) collective-permute-start(bf16[10,18,1,128]{3,2,1,0:T(2,128)(2,1)S(1)} %get-tuple-element.48), channel_id=1, source_target_pairs={{1,0},{3,2},{5,4},{7,6},{9,8},{11,10},{13,12},{15,14},{17,16},{19,... | collective-permute-start | bytes 138248 | tf_op jit(solution)/shard_map/ppermute | solution.py:17
  48.7 6.4 %collective-permute-start.8 = (bf16[6,1,8,128]{3,2,1,0:T(8,128)(2,1)S(1)}, bf16[6,1,8,128]{3,2,1,0:T(8,128)(2,1)S(1)}, u32[]{:S(2)}, u32[]{:S(2)}) collective-permute-start(bf16[6,1,8,128]{3,2,1,0:T(8,128)(2,1)S(1)} %get-tuple-element.172), channel_id=1, source_target_pairs={{0,2},{2,4},{4,6},{1,3},{3,5},{5,7},{8,10},{10,12},{12,14},{9,11},... | collective-permute-start | bytes 36872 | tf_op jit(solution)/shard_map/ppermute | solution.py:15
  53.2 5.0 %collective-permute-start.9 = (bf16[6,1,8,128]{3,2,1,0:T(8,128)(2,1)S(1)}, bf16[6,1,8,128]{3,2,1,0:T(8,128)(2,1)S(1)}, u32[]{:S(2)}, u32[]{:S(2)}) collective-permute-start(bf16[6,1,8,128]{3,2,1,0:T(8,128)(2,1)S(1)} %get-tuple-element.173), channel_id=1, source_target_pairs={{2,0},{4,2},{6,4},{3,1},{5,3},{7,5},{10,8},{12,10},{14,12},{11,9},... | collective-permute-start | bytes 36872 | tf_op jit(solution)/shard_map/ppermute | solution.py:17
  58.3 5.6 %collective-permute-start.10 = (bf16[6,10,1,128]{3,2,1,0:T(2,128)(2,1)S(1)}, bf16[6,10,1,128]{3,2,1,0:T(2,128)(2,1)S(1)}, u32[]{:S(2)}, u32[]{:S(2)}) collective-permute-start(bf16[6,10,1,128]{3,2,1,0:T(2,128)(2,1)S(1)} %get-tuple-element.157), channel_id=1, source_target_pairs={{0,1},{2,3},{4,5},{6,7},{8,9},{10,11},{12,13},{14,15},{16,17},{18,... | collective-permute-start | bytes 46088 | tf_op jit(solution)/shard_map/ppermute | solution.py:15
  59.6 5.0 %collective-permute-start.11 = (bf16[6,10,1,128]{3,2,1,0:T(2,128)(2,1)S(1)}, bf16[6,10,1,128]{3,2,1,0:T(2,128)(2,1)S(1)}, u32[]{:S(2)}, u32[]{:S(2)}) collective-permute-start(bf16[6,10,1,128]{3,2,1,0:T(2,128)(2,1)S(1)} %get-tuple-element.158), channel_id=1, source_target_pairs={{1,0},{3,2},{5,4},{7,6},{9,8},{11,10},{13,12},{15,14},{17,16},{19,... | collective-permute-start | bytes 46088 | tf_op jit(solution)/shard_map/ppermute | solution.py:17
  80.1 8.0 %collective-permute-start.12 = (bf16[8,1,4,256]{3,2,1,0:T(4,128)(2,1)S(1)}, bf16[8,1,4,256]{3,2,1,0:T(4,128)(2,1)S(1)}, u32[]{:S(2)}, u32[]{:S(2)}) collective-permute-start(bf16[8,1,4,256]{3,2,1,0:T(4,128)(2,1)S(1)} %get-tuple-element.178), channel_id=1, source_target_pairs={{0,2},{2,4},{4,6},{1,3},{3,5},{5,7},{8,10},{10,12},{12,14},{9,11},... | collective-permute-start | bytes 49160 | tf_op jit(solution)/shard_map/ppermute | solution.py:15
  86.0 5.2 %collective-permute-start.13 = (bf16[8,1,4,256]{3,2,1,0:T(4,128)(2,1)S(1)}, bf16[8,1,4,256]{3,2,1,0:T(4,128)(2,1)S(1)}, u32[]{:S(2)}, u32[]{:S(2)}) collective-permute-start(bf16[8,1,4,256]{3,2,1,0:T(4,128)(2,1)S(1)} %get-tuple-element.177), channel_id=1, source_target_pairs={{2,0},{4,2},{6,4},{3,1},{5,3},{7,5},{10,8},{12,10},{14,12},{11,9},... | collective-permute-start | bytes 49160 | tf_op jit(solution)/shard_map/ppermute | solution.py:17
  91.5 6.5 %collective-permute-start.14 = (bf16[8,6,1,256]{3,2,1,0:T(2,128)(2,1)S(1)}, bf16[8,6,1,256]{3,2,1,0:T(2,128)(2,1)S(1)}, u32[]{:S(2)}, u32[]{:S(2)}) collective-permute-start(bf16[8,6,1,256]{3,2,1,0:T(2,128)(2,1)S(1)} %get-tuple-element.168), channel_id=1, source_target_pairs={{0,1},{2,3},{4,5},{6,7},{8,9},{10,11},{12,13},{14,15},{16,17},{18,... | collective-permute-start | bytes 73736 | tf_op jit(solution)/shard_map/ppermute | solution.py:15
  92.9 5.2 %collective-permute-start.15 = (bf16[8,6,1,256]{3,2,1,0:T(2,128)(2,1)S(1)}, bf16[8,6,1,256]{3,2,1,0:T(2,128)(2,1)S(1)}, u32[]{:S(2)}, u32[]{:S(2)}) collective-permute-start(bf16[8,6,1,256]{3,2,1,0:T(2,128)(2,1)S(1)} %get-tuple-element.169), channel_id=1, source_target_pairs={{1,0},{3,2},{5,4},{7,6},{9,8},{11,10},{13,12},{15,14},{17,16},{19,... | collective-permute-start | bytes 73736 | tf_op jit(solution)/shard_map/ppermute | solution.py:17
  121.1 6.7 %collective-permute-start.16 = (bf16[8,1,4,512]{3,2,1,0:T(4,128)(2,1)S(1)}, bf16[8,1,4,512]{3,2,1,0:T(4,128)(2,1)S(1)}, u32[]{:S(2)}, u32[]{:S(2)}) collective-permute-start(bf16[8,1,4,512]{3,2,1,0:T(4,128)(2,1)S(1)} %get-tuple-element.154), channel_id=1, source_target_pairs={{0,2},{2,4},{4,6},{1,3},{3,5},{5,7},{8,10},{10,12},{12,14},{9,11},... | collective-permute-start | bytes 98312 | tf_op jit(solution)/shard_map/ppermute | solution.py:15
  125.9 5.2 %collective-permute-start.17 = (bf16[8,1,4,512]{3,2,1,0:T(4,128)(2,1)S(1)}, bf16[8,1,4,512]{3,2,1,0:T(4,128)(2,1)S(1)}, u32[]{:S(2)}, u32[]{:S(2)}) collective-permute-start(bf16[8,1,4,512]{3,2,1,0:T(4,128)(2,1)S(1)} %get-tuple-element.153), channel_id=1, source_target_pairs={{2,0},{4,2},{6,4},{3,1},{5,3},{7,5},{10,8},{12,10},{14,12},{11,9},... | collective-permute-start | bytes 98312 | tf_op jit(solution)/shard_map/ppermute | solution.py:17
  131.5 7.1 %collective-permute-start.18 = (bf16[8,6,1,512]{3,2,1,0:T(2,128)(2,1)S(1)}, bf16[8,6,1,512]{3,2,1,0:T(2,128)(2,1)S(1)}, u32[]{:S(2)}, u32[]{:S(2)}) collective-permute-start(bf16[8,6,1,512]{3,2,1,0:T(2,128)(2,1)S(1)} %get-tuple-element.142), channel_id=1, source_target_pairs={{0,1},{2,3},{4,5},{6,7},{8,9},{10,11},{12,13},{14,15},{16,17},{18,... | collective-permute-start | bytes 147464 | tf_op jit(solution)/shard_map/ppermute | solution.py:15
  132.8 5.8 %collective-permute-start.19 = (bf16[8,6,1,512]{3,2,1,0:T(2,128)(2,1)S(1)}, bf16[8,6,1,512]{3,2,1,0:T(2,128)(2,1)S(1)}, u32[]{:S(2)}, u32[]{:S(2)}) collective-permute-start(bf16[8,6,1,512]{3,2,1,0:T(2,128)(2,1)S(1)} %get-tuple-element.143), channel_id=1, source_target_pairs={{1,0},{3,2},{5,4},{7,6},{9,8},{11,10},{13,12},{15,14},{17,16},{19,... | collective-permute-start | bytes 147464 | tf_op jit(solution)/shard_map/ppermute | solution.py:17
  183.8 5.0 %collective-permute-start.20 = (bf16[1,8,8,768]{3,2,1,0:T(8,128)(2,1)S(1)}, bf16[1,8,8,768]{3,2,1,0:T(8,128)(2,1)S(1)}, u32[]{:S(2)}, u32[]{:S(2)}) collective-permute-start(bf16[1,8,8,768]{3,2,1,0:T(8,128)(2,1)S(1)} %get-tuple-element.95), channel_id=1, source_target_pairs={{0,8},{8,16},{16,24},{1,9},{9,17},{17,25},{2,10},{10,18},{18,26},{... | collective-permute-start | bytes 294920 | tf_op jit(solution)/shard_map/ppermute | solution.py:15
  186.1 6.4 %collective-permute-start.21 = (bf16[1,8,8,768]{3,2,1,0:T(8,128)(2,1)S(1)}, bf16[1,8,8,768]{3,2,1,0:T(8,128)(2,1)S(1)}, u32[]{:S(2)}, u32[]{:S(2)}) collective-permute-start(bf16[1,8,8,768]{3,2,1,0:T(8,128)(2,1)S(1)} %get-tuple-element.96), channel_id=1, source_target_pairs={{8,0},{16,8},{24,16},{9,1},{17,9},{25,17},{10,2},{18,10},{26,18},{... | collective-permute-start | bytes 294920 | tf_op jit(solution)/shard_map/ppermute | solution.py:17
  193.9 7.3 %collective-permute-start.22 = (bf16[6,1,8,768]{3,2,1,0:T(8,128)(2,1)S(1)}, bf16[6,1,8,768]{3,2,1,0:T(8,128)(2,1)S(1)}, u32[]{:S(2)}, u32[]{:S(2)}) collective-permute-start(bf16[6,1,8,768]{3,2,1,0:T(8,128)(2,1)S(1)} %get-tuple-element.68), channel_id=1, source_target_pairs={{0,2},{2,4},{4,6},{1,3},{3,5},{5,7},{8,10},{10,12},{12,14},{9,11},... | collective-permute-start | bytes 221192 | tf_op jit(solution)/shard_map/ppermute | solution.py:15
  197.9 5.7 %collective-permute-start.23 = (bf16[6,1,8,768]{3,2,1,0:T(8,128)(2,1)S(1)}, bf16[6,1,8,768]{3,2,1,0:T(8,128)(2,1)S(1)}, u32[]{:S(2)}, u32[]{:S(2)}) collective-permute-start(bf16[6,1,8,768]{3,2,1,0:T(8,128)(2,1)S(1)} %get-tuple-element.69), channel_id=1, source_target_pairs={{2,0},{4,2},{6,4},{3,1},{5,3},{7,5},{10,8},{12,10},{14,12},{11,9},... | collective-permute-start | bytes 221192 | tf_op jit(solution)/shard_map/ppermute | solution.py:17
  203.8 13.8 %collective-permute-start.24 = (bf16[6,10,1,768]{3,2,1,0:T(2,128)(2,1)S(1)}, bf16[6,10,1,768]{3,2,1,0:T(2,128)(2,1)S(1)}, u32[]{:S(2)}, u32[]{:S(2)}) collective-permute-start(bf16[6,10,1,768]{3,2,1,0:T(2,128)(2,1)S(1)} %get-tuple-element.44), channel_id=1, source_target_pairs={{0,1},{2,3},{4,5},{6,7},{8,9},{10,11},{12,13},{14,15},{16,17},{18,... | collective-permute-start | bytes 276488 | tf_op jit(solution)/shard_map/ppermute | solution.py:15
  205.1 12.5 %collective-permute-start.25 = (bf16[6,10,1,768]{3,2,1,0:T(2,128)(2,1)S(1)}, bf16[6,10,1,768]{3,2,1,0:T(2,128)(2,1)S(1)}, u32[]{:S(2)}, u32[]{:S(2)}) collective-permute-start(bf16[6,10,1,768]{3,2,1,0:T(2,128)(2,1)S(1)} %get-tuple-element.43), channel_id=1, source_target_pairs={{1,0},{3,2},{5,4},{7,6},{9,8},{11,10},{13,12},{15,14},{17,16},{19,... | collective-permute-start | bytes 276488 | tf_op jit(solution)/shard_map/ppermute | solution.py:17
  (16 other events, 97.2 us)
where the time goes:
time: 228 us; the launch traced here: 226 us
  starting transfers between devices  73.7 us (32%)
  matrix products  69.5 us (30%)
  waiting for transfers between devices  27.9 us (12%)
  blocking collectives  25.6 us (11%)
  local copies, waits for them, and re-layouts  16.5 us (7%)
  other arithmetic  10.6 us (5%)
    dot_general x135, matrix products, convolve(): jnp.dot(window.reshape(-1, channels), kernel[offset_x, offset_y, offset_z...  69.5 us
    ppermute x13, starting transfers between devices, with_halo(): lax.ppermute(tail, axis, [(i, (i + 1) % count) for i in range(ends)])  39.6 us
    ppermute x13, starting transfers between devices, with_halo(): lax.ppermute(head, axis, [((i + 1) % count, i) for i in range(ends)])  34 us
    ppermute x13, waiting for transfers between devices, with_halo(): lax.ppermute(head, axis, [((i + 1) % count, i) for i in range(ends)])  27.8 us
    all_gather x1, blocking collectives, on_device(): column = lax.all_gather(coarse, 'gx', axis=0, tiled=True)  10.3 us
    concatenate x16, other arithmetic, with_halo(): jnp.concatenate([lax.ppermute(tail, axis, [(i, (i + 1) % count) for i in...  9.53 us
    all_gather x1, blocking collectives, on_device(): filters = lax.all_gather(bottom_first, 'gx', axis=3, tiled=True)  8.49 us
    reshape x54, local copies, waits for them, and re-layouts, convolve(): window.reshape(-1, channels)  7.16 us
  transfers between devices with their start and end apart: 26, of which 11 were waited for; matrix products, arithmetic and copies ran while one was open for 6% of the time, Pallas kernels for 0%

commit v1 on v0

--- a/solution.py
+++ b/solution.py
@@ -79,7 +79,15 @@
     filters = lax.all_gather(bottom_first, "gx", axis=3, tiled=True)
     filters = with_halo(filters, (("gy", 1), ("gz", 2)), 1)
     bottom_second = rectify(convolve(pad_first(filters), w_bottom_out))
-    regrouped = lax.all_to_all(bottom_second, "gx", split_axis=0, concat_axis=3, tiled=True)
+    regrouped = jnp.concatenate(
+        lax.all_to_all(
+            jnp.stack(jnp.split(bottom_second, lax.axis_size("gx"), 0), axis=0),
+            axis_name="gx",
+            split_axis=0,
+            concat_axis=0,
+        ),
+        3,
+    )
     joined = jnp.concatenate([enlarge(regrouped), skip_level], axis=3)
     joined = with_halo(joined, (("gx", 0), ("gy", 1), ("gz", 2)), 1)
     return convolve(joined, w_up).astype(jnp.bfloat16)

time: 228 us -> 228 us (level)
  no operation moved by 1% of the time
where the time goes in v1:
time: 228 us; the launch traced here: 226 us
  starting transfers between devices  73.6 us (32%)
  matrix products  69.5 us (30%)
  waiting for transfers between devices  27.9 us (12%)
  blocking collectives  25.6 us (11%)
  local copies, waits for them, and re-layouts  16.4 us (7%)
  other arithmetic  10.6 us (5%)
    dot_general x135, matrix products, convolve(): jnp.dot(window.reshape(-1, channels), kernel[offset_x, offset_y, offset_z...  69.5 us
    ppermute x13, starting transfers between devices, with_halo(): lax.ppermute(tail, axis, [(i, (i + 1) % count) for i in range(ends)])  39.6 us
    ppermute x13, starting transfers between devices, with_halo(): lax.ppermute(head, axis, [((i + 1) % count, i) for i in range(ends)])  34 us
    ppermute x13, waiting for transfers between devices, with_halo(): lax.ppermute(head, axis, [((i + 1) % count, i) for i in range(ends)])  27.8 us
    all_gather x1, blocking collectives, on_device(): column = lax.all_gather(coarse, 'gx', axis=0, tiled=True)  10.3 us
    concatenate x16, other arithmetic, with_halo(): jnp.concatenate([lax.ppermute(tail, axis, [(i, (i + 1) % count) for i in...  9.54 us
    all_gather x1, blocking collectives, on_device(): filters = lax.all_gather(bottom_first, 'gx', axis=3, tiled=True)  8.49 us
    reshape x54, local copies, waits for them, and re-layouts, convolve(): window.reshape(-1, channels)  7.1 us
  transfers between devices with their start and end apart: 26, of which 11 were waited for; matrix products, arithmetic and copies ran while one was open for 6% of the time, Pallas kernels for 0%

profile of v1, /device:TPU:3, one launch (start us, length us, event | category | flops | bytes accessed | tf_op | source)
XLA Modules:
  0.0 225.6 jit_solution(5815712846739366740)
XLA Ops:
  0.9 3.2 %collective-permute-start = (bf16[1,16,16,128]{3,2,1,0:T(8,128)(2,1)S(1)}, bf16[1,16,16,128]{3,2,1,0:T(8,128)(2,1)S(1)}, u32[]{:S(2)}, u32[]{:S(2)}) collective-permute-start(bf16[1,16,16,128]{3,2,1,0:T(8,128)(2,1)S(1)} %get-tuple-element.74), channel_id=1, source_target_pairs={{0,8},{8,16},{16,24},{1,9},{9,17},{17,25},{2,10},{10,18},{18,26},{... | collective-permute-start | bytes 196616 | tf_op jit(solution)/shard_map/ppermute | solution.py:15
  5.4 3.7 %collective-permute-done.1 = bf16[1,16,16,128]{3,2,1,0:T(8,128)(2,1)S(1)} collective-permute-done((bf16[1,16,16,128]{3,2,1,0:T(8,128)(2,1)S(1)}, bf16[1,16,16,128]{3,2,1,0:T(8,128)(2,1)S(1)}, u32[]{:S(2)}, u32[]{:S(2)}) %collective-permute-start.1) | collective-permute-done | bytes 65568 | tf_op jit(solution)/shard_map/ppermute | solution.py:17
  11.0 5.1 %collective-permute-start.2 = (bf16[10,1,16,128]{3,2,1,0:T(8,128)(2,1)S(1)}, bf16[10,1,16,128]{3,2,1,0:T(8,128)(2,1)S(1)}, u32[]{:S(2)}, u32[]{:S(2)}) collective-permute-start(bf16[10,1,16,128]{3,2,1,0:T(8,128)(2,1)S(1)} %get-tuple-element.64), channel_id=1, source_target_pairs={{0,2},{2,4},{4,6},{1,3},{3,5},{5,7},{8,10},{10,12},{12,14},{9,11},... | collective-permute-start | bytes 122888 | tf_op jit(solution)/shard_map/ppermute | solution.py:15
  18.1 3.4 %collective-permute-done.3 = bf16[10,1,16,128]{3,2,1,0:T(8,128)(2,1)S(1)} collective-permute-done((bf16[10,1,16,128]{3,2,1,0:T(8,128)(2,1)S(1)}, bf16[10,1,16,128]{3,2,1,0:T(8,128)(2,1)S(1)}, u32[]{:S(2)}, u32[]{:S(2)}) %collective-permute-start.3) | collective-permute-done | bytes 40992 | tf_op jit(solution)/shard_map/ppermute | solution.py:17
  22.9 4.1 %collective-permute-start.5 = (bf16[10,18,1,128]{3,2,1,0:T(2,128)(2,1)S(1)}, bf16[10,18,1,128]{3,2,1,0:T(2,128)(2,1)S(1)}, u32[]{:S(2)}, u32[]{:S(2)}) collective-permute-start(bf16[10,18,1,128]{3,2,1,0:T(2,128)(2,1)S(1)} %get-tuple-element.48), channel_id=1, source_target_pairs={{1,0},{3,2},{5,4},{7,6},{9,8},{11,10},{13,12},{15,14},{17,16},{19,... | collective-permute-start | bytes 138248 | tf_op jit(solution)/shard_map/ppermute | solution.py:17
  29.5 2.6 %fusion.380 = (bf16[8,16,16,128]{3,2,1,0:T(8,128)(2,1)S(1)}, bf16[8,16,16,128]{3,2,1,0:T(8,128)(2,1)S(1)}, bf16[8,16,16,128]{3,2,1,0:T(8,128)(2,1)S(1)}, bf16[8,...) fusion(bf16[10,18,17,128]{3,2,1,0:T(8,128)(2,1)S(1)} %get-tuple, ...), kind=kLoop, calls=%fused_computation.567 | loop fusion | bytes 18874368 | tf_op jit(solution)/shard_map/slice | solution.py:33
  41.0 3.2 %collective-permute-start.6 = (bf16[1,8,8,128]{3,2,1,0:T(8,128)(2,1)S(1)}, bf16[1,8,8,128]{3,2,1,0:T(8,128)(2,1)S(1)}, u32[]{:S(2)}, u32[]{:S(2)}) collective-permute-start(bf16[1,8,8,128]{3,2,1,0:T(8,128)(2,1)S(1)} %get-tuple-element.181), channel_id=1, source_target_pairs={{0,8},{8,16},{16,24},{1,9},{9,17},{17,25},{2,10},{10,18},{18,26},{... | collective-permute-start | bytes 49160 | tf_op jit(solution)/shard_map/ppermute | solution.py:15
  45.6 3.2 %collective-permute-done.7 = bf16[1,8,8,128]{3,2,1,0:T(8,128)(2,1)S(1)} collective-permute-done((bf16[1,8,8,128]{3,2,1,0:T(8,128)(2,1)S(1)}, bf16[1,8,8,128]{3,2,1,0:T(8,128)(2,1)S(1)}, u32[]{:S(2)}, u32[]{:S(2)}) %collective-permute-start.7) | collective-permute-done | bytes 16416 | tf_op jit(solution)/shard_map/ppermute | solution.py:17
  48.7 4.4 %collective-permute-start.8 = (bf16[6,1,8,128]{3,2,1,0:T(8,128)(2,1)S(1)}, bf16[6,1,8,128]{3,2,1,0:T(8,128)(2,1)S(1)}, u32[]{:S(2)}, u32[]{:S(2)}) collective-permute-start(bf16[6,1,8,128]{3,2,1,0:T(8,128)(2,1)S(1)} %get-tuple-element.172), channel_id=1, source_target_pairs={{0,2},{2,4},{4,6},{1,3},{3,5},{5,7},{8,10},{10,12},{12,14},{9,11},... | collective-permute-start | bytes 36872 | tf_op jit(solution)/shard_map/ppermute | solution.py:15
  55.2 3.1 %collective-permute-done.9 = bf16[6,1,8,128]{3,2,1,0:T(8,128)(2,1)S(1)} collective-permute-done((bf16[6,1,8,128]{3,2,1,0:T(8,128)(2,1)S(1)}, bf16[6,1,8,128]{3,2,1,0:T(8,128)(2,1)S(1)}, u32[]{:S(2)}, u32[]{:S(2)}) %collective-permute-start.9) | collective-permute-done | bytes 12320 | tf_op jit(solution)/shard_map/ppermute | solution.py:17
  59.6 4.0 %collective-permute-start.11 = (bf16[6,10,1,128]{3,2,1,0:T(2,128)(2,1)S(1)}, bf16[6,10,1,128]{3,2,1,0:T(2,128)(2,1)S(1)}, u32[]{:S(2)}, u32[]{:S(2)}) collective-permute-start(bf16[6,10,1,128]{3,2,1,0:T(2,128)(2,1)S(1)} %get-tuple-element.158), channel_id=1, source_target_pairs={{1,0},{3,2},{5,4},{7,6},{9,8},{11,10},{13,12},{15,14},{17,16},{19,... | collective-permute-start | bytes 46088 | tf_op jit(solution)/shard_map/ppermute | solution.py:17
  69.9 10.3 %all_gather.6 = bf16[8,4,4,256]{3,2,1,0:T(4,128)(2,1)S(1)} all-gather(bf16[2,4,4,256]{3,2,1,0:T(4,128)(2,1)S(1)} %reduce_max.19), channel_id=1, replica_groups=mesh['gx'=4,'gy'=4,'gz'=2] {'gx'}, dimensions={0}, use_global_device_ids=true | all-gather | bytes 81920 | tf_op jit(solution)/shard_map/all_gather | solution.py:76
  80.2 5.9 %collective-permute-start.12 = (bf16[8,1,4,256]{3,2,1,0:T(4,128)(2,1)S(1)}, bf16[8,1,4,256]{3,2,1,0:T(4,128)(2,1)S(1)}, u32[]{:S(2)}, u32[]{:S(2)}) collective-permute-start(bf16[8,1,4,256]{3,2,1,0:T(4,128)(2,1)S(1)} %get-tuple-element.178), channel_id=1, source_target_pairs={{0,2},{2,4},{4,6},{1,3},{3,5},{5,7},{8,10},{10,12},{12,14},{9,11},... | collective-permute-start | bytes 49160 | tf_op jit(solution)/shard_map/ppermute | solution.py:15
  88.2 3.1 %collective-permute-done.13 = bf16[8,1,4,256]{3,2,1,0:T(4,128)(2,1)S(1)} collective-permute-done((bf16[8,1,4,256]{3,2,1,0:T(4,128)(2,1)S(1)}, bf16[8,1,4,256]{3,2,1,0:T(4,128)(2,1)S(1)}, u32[]{:S(2)}, u32[]{:S(2)}) %collective-permute-start.13) | collective-permute-done | bytes 16416 | tf_op jit(solution)/shard_map/ppermute | solution.py:17
  92.9 4.0 %collective-permute-start.15 = (bf16[8,6,1,256]{3,2,1,0:T(2,128)(2,1)S(1)}, bf16[8,6,1,256]{3,2,1,0:T(2,128)(2,1)S(1)}, u32[]{:S(2)}, u32[]{:S(2)}) collective-permute-start(bf16[8,6,1,256]{3,2,1,0:T(2,128)(2,1)S(1)} %get-tuple-element.169), channel_id=1, source_target_pairs={{1,0},{3,2},{5,4},{7,6},{9,8},{11,10},{13,12},{15,14},{17,16},{19,... | collective-permute-start | bytes 73736 | tf_op jit(solution)/shard_map/ppermute | solution.py:17
  112.6 8.5 %all_gather.7 = bf16[8,4,4,512]{3,2,1,0:T(4,128)(2,1)S(1)} all-gather(bf16[8,4,4,128]{3,2,1,0:T(4,128)(2,1)S(1)} %bitcast.722), channel_id=1, replica_groups=mesh['gx'=4,'gy'=4,'gz'=2] {'gx'}, dimensions={3}, use_global_device_ids=true | all-gather | bytes 163840 | tf_op jit(solution)/shard_map/all_gather | solution.py:79
  121.1 4.8 %collective-permute-start.16 = (bf16[8,1,4,512]{3,2,1,0:T(4,128)(2,1)S(1)}, bf16[8,1,4,512]{3,2,1,0:T(4,128)(2,1)S(1)}, u32[]{:S(2)}, u32[]{:S(2)}) collective-permute-start(bf16[8,1,4,512]{3,2,1,0:T(4,128)(2,1)S(1)} %get-tuple-element.154), channel_id=1, source_target_pairs={{0,2},{2,4},{4,6},{1,3},{3,5},{5,7},{8,10},{10,12},{12,14},{9,11},... | collective-permute-start | bytes 98312 | tf_op jit(solution)/shard_map/ppermute | solution.py:15
  127.8 3.3 %collective-permute-done.17 = bf16[8,1,4,512]{3,2,1,0:T(4,128)(2,1)S(1)} collective-permute-done((bf16[8,1,4,512]{3,2,1,0:T(4,128)(2,1)S(1)}, bf16[8,1,4,512]{3,2,1,0:T(4,128)(2,1)S(1)}, u32[]{:S(2)}, u32[]{:S(2)}) %collective-permute-start.17) | collective-permute-done | bytes 32800 | tf_op jit(solution)/shard_map/ppermute | solution.py:17
  132.8 4.0 %collective-permute-start.19 = (bf16[8,6,1,512]{3,2,1,0:T(2,128)(2,1)S(1)}, bf16[8,6,1,512]{3,2,1,0:T(2,128)(2,1)S(1)}, u32[]{:S(2)}, u32[]{:S(2)}) collective-permute-start(bf16[8,6,1,512]{3,2,1,0:T(2,128)(2,1)S(1)} %get-tuple-element.143), channel_id=1, source_target_pairs={{1,0},{3,2},{5,4},{7,6},{9,8},{11,10},{13,12},{15,14},{17,16},{19,... | collective-permute-start | bytes 147464 | tf_op jit(solution)/shard_map/ppermute | solution.py:17
  143.5 2.6 %pad_maximum_fusion.20 = (bf16[8,4,4,512]{3,2,1,0:T(4,128)(2,1)S(1)}, bf16[8,4,4,512]{3,2,1,0:T(4,128)(2,1)}, bf16[8,4,4,512]{3,2,1,0:T(4,128)(2,1)S(1)}, bf16[8...) fusion(bf16[8,6,4,512]{3,2,1,0:T(4,128)(2,1)S(1)} %constant_dynamic-update-slice, ...), kind=kLoop, calls=%fused_computation.288 | loop fusion | flops 1572864 | bytes 1081344 | tf_op jit(solution)/shard_map/concatenate | solution.py:13
  176.4 6.9 %all_to_all.5 = bf16[4,2,4,4,128]{4,3,2,1,0:T(4,128)(2,1)S(1)} all-to-all(bf16[4,2,4,4,128]{4,3,2,1,0:T(4,128)(2,1)S(1)} %pad_maximum_fusion.38), channel_id=1, replica_groups=mesh['gx'=4,'gy'=4,'gz'=2] {'gx'}, dimensions={0} | all-to-all | bytes 65536 | tf_op jit(solution)/shard_map/all_to_all | solution.py:83
  188.7 3.8 %collective-permute-done.21 = bf16[1,8,8,768]{3,2,1,0:T(8,128)(2,1)S(1)} collective-permute-done((bf16[1,8,8,768]{3,2,1,0:T(8,128)(2,1)S(1)}, bf16[1,8,8,768]{3,2,1,0:T(8,128)(2,1)S(1)}, u32[]{:S(2)}, u32[]{:S(2)}) %collective-permute-start.21) | collective-permute-done | bytes 98336 | tf_op jit(solution)/shard_map/ppermute | solution.py:17
  193.8 4.0 %collective-permute-start.22 = (bf16[6,1,8,768]{3,2,1,0:T(8,128)(2,1)S(1)}, bf16[6,1,8,768]{3,2,1,0:T(8,128)(2,1)S(1)}, u32[]{:S(2)}, u32[]{:S(2)}) collective-permute-start(bf16[6,1,8,768]{3,2,1,0:T(8,128)(2,1)S(1)} %get-tuple-element.68), channel_id=1, source_target_pairs={{0,2},{2,4},{4,6},{1,3},{3,5},{5,7},{8,10},{10,12},{12,14},{9,11},... | collective-permute-start | bytes 221192 | tf_op jit(solution)/shard_map/ppermute | solution.py:15
  205.1 4.2 %collective-permute-start.25 = (bf16[6,10,1,768]{3,2,1,0:T(2,128)(2,1)S(1)}, bf16[6,10,1,768]{3,2,1,0:T(2,128)(2,1)S(1)}, u32[]{:S(2)}, u32[]{:S(2)}) collective-permute-start(bf16[6,10,1,768]{3,2,1,0:T(2,128)(2,1)S(1)} %get-tuple-element.43), channel_id=1, source_target_pairs={{1,0},{3,2},{5,4},{7,6},{9,8},{11,10},{13,12},{15,14},{17,16},{19,... | collective-permute-start | bytes 276488 | tf_op jit(solution)/shard_map/ppermute | solution.py:17
  (303 shorter events, 118.5 us)
Async XLA Ops:
  0.9 4.5 %collective-permute-start = (bf16[1,16,16,128]{3,2,1,0:T(8,128)(2,1)S(1)}, bf16[1,16,16,128]{3,2,1,0:T(8,128)(2,1)S(1)}, u32[]{:S(2)}, u32[]{:S(2)}) collective-permute-start(bf16[1,16,16,128]{3,2,1,0:T(8,128)(2,1)S(1)} %get-tuple-element.74), channel_id=1, source_target_pairs={{0,8},{8,16},{16,24},{1,9},{9,17},{17,25},{2,10},{10,18},{18,26},{... | collective-permute-start | bytes 196616 | tf_op jit(solution)/shard_map/ppermute | solution.py:15
  4.1 5.0 %collective-permute-start.1 = (bf16[1,16,16,128]{3,2,1,0:T(8,128)(2,1)S(1)}, bf16[1,16,16,128]{3,2,1,0:T(8,128)(2,1)S(1)}, u32[]{:S(2)}, u32[]{:S(2)}) collective-permute-start(bf16[1,16,16,128]{3,2,1,0:T(8,128)(2,1)S(1)} %get-tuple-element.73), channel_id=1, source_target_pairs={{8,0},{16,8},{24,16},{9,1},{17,9},{25,17},{10,2},{18,10},{26,18},{... | collective-permute-start | bytes 196616 | tf_op jit(solution)/shard_map/ppermute | solution.py:17
  11.0 7.1 %collective-permute-start.2 = (bf16[10,1,16,128]{3,2,1,0:T(8,128)(2,1)S(1)}, bf16[10,1,16,128]{3,2,1,0:T(8,128)(2,1)S(1)}, u32[]{:S(2)}, u32[]{:S(2)}) collective-permute-start(bf16[10,1,16,128]{3,2,1,0:T(8,128)(2,1)S(1)} %get-tuple-element.64), channel_id=1, source_target_pairs={{0,2},{2,4},{4,6},{1,3},{3,5},{5,7},{8,10},{10,12},{12,14},{9,11},... | collective-permute-start | bytes 122888 | tf_op jit(solution)/shard_map/ppermute | solution.py:15
  16.1 5.3 %collective-permute-start.3 = (bf16[10,1,16,128]{3,2,1,0:T(8,128)(2,1)S(1)}, bf16[10,1,16,128]{3,2,1,0:T(8,128)(2,1)S(1)}, u32[]{:S(2)}, u32[]{:S(2)}) collective-permute-start(bf16[10,1,16,128]{3,2,1,0:T(8,128)(2,1)S(1)} %get-tuple-element.65), channel_id=1, source_target_pairs={{2,0},{4,2},{6,4},{3,1},{5,3},{7,5},{10,8},{12,10},{14,12},{11,9},... | collective-permute-start | bytes 122888 | tf_op jit(solution)/shard_map/ppermute | solution.py:17
  21.6 5.9 %collective-permute-start.4 = (bf16[10,18,1,128]{3,2,1,0:T(2,128)(2,1)S(1)}, bf16[10,18,1,128]{3,2,1,0:T(2,128)(2,1)S(1)}, u32[]{:S(2)}, u32[]{:S(2)}) collective-permute-start(bf16[10,18,1,128]{3,2,1,0:T(2,128)(2,1)S(1)} %get-tuple-element.47), channel_id=1, source_target_pairs={{0,1},{2,3},{4,5},{6,7},{8,9},{10,11},{12,13},{14,15},{16,17},{18,... | collective-permute-start | bytes 138248 | tf_op jit(solution)/shard_map/ppermute | solution.py:15
  22.9 5.7 %collective-permute-start.5 = (bf16[10,18,1,128]{3,2,1,0:T(2,128)(2,1)S(1)}, bf16[10,18,1,128]{3,2,1,0:T(2,128)(2,1)S(1)}, u32[]{:S(2)}, u32[]{:S(2)}) collective-permute-start(bf16[10,18,1,128]{3,2,1,0:T(2,128)(2,1)S(1)} %get-tuple-element.48), channel_id=1, source_target_pairs={{1,0},{3,2},{5,4},{7,6},{9,8},{11,10},{13,12},{15,14},{17,16},{19,... | collective-permute-start | bytes 138248 | tf_op jit(solution)/shard_map/ppermute | solution.py:17
  48.7 6.4 %collective-permute-start.8 = (bf16[6,1,8,128]{3,2,1,0:T(8,128)(2,1)S(1)}, bf16[6,1,8,128]{3,2,1,0:T(8,128)(2,1)S(1)}, u32[]{:S(2)}, u32[]{:S(2)}) collective-permute-start(bf16[6,1,8,128]{3,2,1,0:T(8,128)(2,1)S(1)} %get-tuple-element.172), channel_id=1, source_target_pairs={{0,2},{2,4},{4,6},{1,3},{3,5},{5,7},{8,10},{10,12},{12,14},{9,11},... | collective-permute-start | bytes 36872 | tf_op jit(solution)/shard_map/ppermute | solution.py:15
  53.2 5.0 %collective-permute-start.9 = (bf16[6,1,8,128]{3,2,1,0:T(8,128)(2,1)S(1)}, bf16[6,1,8,128]{3,2,1,0:T(8,128)(2,1)S(1)}, u32[]{:S(2)}, u32[]{:S(2)}) collective-permute-start(bf16[6,1,8,128]{3,2,1,0:T(8,128)(2,1)S(1)} %get-tuple-element.173), channel_id=1, source_target_pairs={{2,0},{4,2},{6,4},{3,1},{5,3},{7,5},{10,8},{12,10},{14,12},{11,9},... | collective-permute-start | bytes 36872 | tf_op jit(solution)/shard_map/ppermute | solution.py:17
  58.3 5.6 %collective-permute-start.10 = (bf16[6,10,1,128]{3,2,1,0:T(2,128)(2,1)S(1)}, bf16[6,10,1,128]{3,2,1,0:T(2,128)(2,1)S(1)}, u32[]{:S(2)}, u32[]{:S(2)}) collective-permute-start(bf16[6,10,1,128]{3,2,1,0:T(2,128)(2,1)S(1)} %get-tuple-element.157), channel_id=1, source_target_pairs={{0,1},{2,3},{4,5},{6,7},{8,9},{10,11},{12,13},{14,15},{16,17},{18,... | collective-permute-start | bytes 46088 | tf_op jit(solution)/shard_map/ppermute | solution.py:15
  59.6 5.0 %collective-permute-start.11 = (bf16[6,10,1,128]{3,2,1,0:T(2,128)(2,1)S(1)}, bf16[6,10,1,128]{3,2,1,0:T(2,128)(2,1)S(1)}, u32[]{:S(2)}, u32[]{:S(2)}) collective-permute-start(bf16[6,10,1,128]{3,2,1,0:T(2,128)(2,1)S(1)} %get-tuple-element.158), channel_id=1, source_target_pairs={{1,0},{3,2},{5,4},{7,6},{9,8},{11,10},{13,12},{15,14},{17,16},{19,... | collective-permute-start | bytes 46088 | tf_op jit(solution)/shard_map/ppermute | solution.py:17
  80.2 8.0 %collective-permute-start.12 = (bf16[8,1,4,256]{3,2,1,0:T(4,128)(2,1)S(1)}, bf16[8,1,4,256]{3,2,1,0:T(4,128)(2,1)S(1)}, u32[]{:S(2)}, u32[]{:S(2)}) collective-permute-start(bf16[8,1,4,256]{3,2,1,0:T(4,128)(2,1)S(1)} %get-tuple-element.178), channel_id=1, source_target_pairs={{0,2},{2,4},{4,6},{1,3},{3,5},{5,7},{8,10},{10,12},{12,14},{9,11},... | collective-permute-start | bytes 49160 | tf_op jit(solution)/shard_map/ppermute | solution.py:15
  86.1 5.2 %collective-permute-start.13 = (bf16[8,1,4,256]{3,2,1,0:T(4,128)(2,1)S(1)}, bf16[8,1,4,256]{3,2,1,0:T(4,128)(2,1)S(1)}, u32[]{:S(2)}, u32[]{:S(2)}) collective-permute-start(bf16[8,1,4,256]{3,2,1,0:T(4,128)(2,1)S(1)} %get-tuple-element.177), channel_id=1, source_target_pairs={{2,0},{4,2},{6,4},{3,1},{5,3},{7,5},{10,8},{12,10},{14,12},{11,9},... | collective-permute-start | bytes 49160 | tf_op jit(solution)/shard_map/ppermute | solution.py:17
  91.5 6.5 %collective-permute-start.14 = (bf16[8,6,1,256]{3,2,1,0:T(2,128)(2,1)S(1)}, bf16[8,6,1,256]{3,2,1,0:T(2,128)(2,1)S(1)}, u32[]{:S(2)}, u32[]{:S(2)}) collective-permute-start(bf16[8,6,1,256]{3,2,1,0:T(2,128)(2,1)S(1)} %get-tuple-element.168), channel_id=1, source_target_pairs={{0,1},{2,3},{4,5},{6,7},{8,9},{10,11},{12,13},{14,15},{16,17},{18,... | collective-permute-start | bytes 73736 | tf_op jit(solution)/shard_map/ppermute | solution.py:15
  92.9 5.2 %collective-permute-start.15 = (bf16[8,6,1,256]{3,2,1,0:T(2,128)(2,1)S(1)}, bf16[8,6,1,256]{3,2,1,0:T(2,128)(2,1)S(1)}, u32[]{:S(2)}, u32[]{:S(2)}) collective-permute-start(bf16[8,6,1,256]{3,2,1,0:T(2,128)(2,1)S(1)} %get-tuple-element.169), channel_id=1, source_target_pairs={{1,0},{3,2},{5,4},{7,6},{9,8},{11,10},{13,12},{15,14},{17,16},{19,... | collective-permute-start | bytes 73736 | tf_op jit(solution)/shard_map/ppermute | solution.py:17
  121.1 6.7 %collective-permute-start.16 = (bf16[8,1,4,512]{3,2,1,0:T(4,128)(2,1)S(1)}, bf16[8,1,4,512]{3,2,1,0:T(4,128)(2,1)S(1)}, u32[]{:S(2)}, u32[]{:S(2)}) collective-permute-start(bf16[8,1,4,512]{3,2,1,0:T(4,128)(2,1)S(1)} %get-tuple-element.154), channel_id=1, source_target_pairs={{0,2},{2,4},{4,6},{1,3},{3,5},{5,7},{8,10},{10,12},{12,14},{9,11},... | collective-permute-start | bytes 98312 | tf_op jit(solution)/shard_map/ppermute | solution.py:15
  125.9 5.2 %collective-permute-start.17 = (bf16[8,1,4,512]{3,2,1,0:T(4,128)(2,1)S(1)}, bf16[8,1,4,512]{3,2,1,0:T(4,128)(2,1)S(1)}, u32[]{:S(2)}, u32[]{:S(2)}) collective-permute-start(bf16[8,1,4,512]{3,2,1,0:T(4,128)(2,1)S(1)} %get-tuple-element.153), channel_id=1, source_target_pairs={{2,0},{4,2},{6,4},{3,1},{5,3},{7,5},{10,8},{12,10},{14,12},{11,9},... | collective-permute-start | bytes 98312 | tf_op jit(solution)/shard_map/ppermute | solution.py:17
  131.5 7.1 %collective-permute-start.18 = (bf16[8,6,1,512]{3,2,1,0:T(2,128)(2,1)S(1)}, bf16[8,6,1,512]{3,2,1,0:T(2,128)(2,1)S(1)}, u32[]{:S(2)}, u32[]{:S(2)}) collective-permute-start(bf16[8,6,1,512]{3,2,1,0:T(2,128)(2,1)S(1)} %get-tuple-element.142), channel_id=1, source_target_pairs={{0,1},{2,3},{4,5},{6,7},{8,9},{10,11},{12,13},{14,15},{16,17},{18,... | collective-permute-start | bytes 147464 | tf_op jit(solution)/shard_map/ppermute | solution.py:15
  132.8 5.8 %collective-permute-start.19 = (bf16[8,6,1,512]{3,2,1,0:T(2,128)(2,1)S(1)}, bf16[8,6,1,512]{3,2,1,0:T(2,128)(2,1)S(1)}, u32[]{:S(2)}, u32[]{:S(2)}) collective-permute-start(bf16[8,6,1,512]{3,2,1,0:T(2,128)(2,1)S(1)} %get-tuple-element.143), channel_id=1, source_target_pairs={{1,0},{3,2},{5,4},{7,6},{9,8},{11,10},{13,12},{15,14},{17,16},{19,... | collective-permute-start | bytes 147464 | tf_op jit(solution)/shard_map/ppermute | solution.py:17
  183.7 5.0 %collective-permute-start.20 = (bf16[1,8,8,768]{3,2,1,0:T(8,128)(2,1)S(1)}, bf16[1,8,8,768]{3,2,1,0:T(8,128)(2,1)S(1)}, u32[]{:S(2)}, u32[]{:S(2)}) collective-permute-start(bf16[1,8,8,768]{3,2,1,0:T(8,128)(2,1)S(1)} %get-tuple-element.95), channel_id=1, source_target_pairs={{0,8},{8,16},{16,24},{1,9},{9,17},{17,25},{2,10},{10,18},{18,26},{... | collective-permute-start | bytes 294920 | tf_op jit(solution)/shard_map/ppermute | solution.py:15
  186.1 6.4 %collective-permute-start.21 = (bf16[1,8,8,768]{3,2,1,0:T(8,128)(2,1)S(1)}, bf16[1,8,8,768]{3,2,1,0:T(8,128)(2,1)S(1)}, u32[]{:S(2)}, u32[]{:S(2)}) collective-permute-start(bf16[1,8,8,768]{3,2,1,0:T(8,128)(2,1)S(1)} %get-tuple-element.96), channel_id=1, source_target_pairs={{8,0},{16,8},{24,16},{9,1},{17,9},{25,17},{10,2},{18,10},{26,18},{... | collective-permute-start | bytes 294920 | tf_op jit(solution)/shard_map/ppermute | solution.py:17
  193.8 7.2 %collective-permute-start.22 = (bf16[6,1,8,768]{3,2,1,0:T(8,128)(2,1)S(1)}, bf16[6,1,8,768]{3,2,1,0:T(8,128)(2,1)S(1)}, u32[]{:S(2)}, u32[]{:S(2)}) collective-permute-start(bf16[6,1,8,768]{3,2,1,0:T(8,128)(2,1)S(1)} %get-tuple-element.68), channel_id=1, source_target_pairs={{0,2},{2,4},{4,6},{1,3},{3,5},{5,7},{8,10},{10,12},{12,14},{9,11},... | collective-permute-start | bytes 221192 | tf_op jit(solution)/shard_map/ppermute | solution.py:15
  197.8 5.7 %collective-permute-start.23 = (bf16[6,1,8,768]{3,2,1,0:T(8,128)(2,1)S(1)}, bf16[6,1,8,768]{3,2,1,0:T(8,128)(2,1)S(1)}, u32[]{:S(2)}, u32[]{:S(2)}) collective-permute-start(bf16[6,1,8,768]{3,2,1,0:T(8,128)(2,1)S(1)} %get-tuple-element.69), channel_id=1, source_target_pairs={{2,0},{4,2},{6,4},{3,1},{5,3},{7,5},{10,8},{12,10},{14,12},{11,9},... | collective-permute-start | bytes 221192 | tf_op jit(solution)/shard_map/ppermute | solution.py:17
  203.8 13.8 %collective-permute-start.24 = (bf16[6,10,1,768]{3,2,1,0:T(2,128)(2,1)S(1)}, bf16[6,10,1,768]{3,2,1,0:T(2,128)(2,1)S(1)}, u32[]{:S(2)}, u32[]{:S(2)}) collective-permute-start(bf16[6,10,1,768]{3,2,1,0:T(2,128)(2,1)S(1)} %get-tuple-element.44), channel_id=1, source_target_pairs={{0,1},{2,3},{4,5},{6,7},{8,9},{10,11},{12,13},{14,15},{16,17},{18,... | collective-permute-start | bytes 276488 | tf_op jit(solution)/shard_map/ppermute | solution.py:15
  205.1 12.5 %collective-permute-start.25 = (bf16[6,10,1,768]{3,2,1,0:T(2,128)(2,1)S(1)}, bf16[6,10,1,768]{3,2,1,0:T(2,128)(2,1)S(1)}, u32[]{:S(2)}, u32[]{:S(2)}) collective-permute-start(bf16[6,10,1,768]{3,2,1,0:T(2,128)(2,1)S(1)} %get-tuple-element.43), channel_id=1, source_target_pairs={{1,0},{3,2},{5,4},{7,6},{9,8},{11,10},{13,12},{15,14},{17,16},{19,... | collective-permute-start | bytes 276488 | tf_op jit(solution)/shard_map/ppermute | solution.py:17
  (16 other events, 97.2 us)
